TPU v7x, 32 devices: a whole 2x2x4 slice. The times are simulated.
32 devices in a mesh: rep: 1, dp: 32 (over x, y, z, core).
Axes of the slice: x: 2, y: 2, z: 4, core: 2. Of those that a mesh axis runs over, the one named last changes fastest.
Arguments:
- a: bfloat16 [32, 2, 4096, 1024], P(('rep', 'dp'))
- g: bfloat16 [32, 2, 4096, 3200], P(('rep', 'dp'))
Outputs:
- output: bfloat16 [2, 1024, 3200], P('rep')
All inputs are finite; a program needn't handle non-finite values.
Results may differ from a plain program's by a relative error of at most 0.012.
Values are sent between devices in bfloat16 or wider.
A program may use at most 2 GiB of HBM per device.

v0:
```python
import jax
import jax.numpy as jnp


def solution(mesh):
    groups = mesh.shape["rep"]

    def step(a, g):
        a, g = (t.reshape(groups, -1, *t.shape[1:]) for t in (a, g))
        sums = jnp.einsum("rsntd,rsntf->rndf", a, g, preferred_element_type=jnp.float32)
        return sums.astype(jnp.bfloat16).reshape(-1, *sums.shape[2:])

    return step
```

profile of v0, /device:TPU:0, one launch (start us, length us, event | category | flops | bytes accessed | tf_op | source)
XLA Modules:
  0.0 488.9 jit_solution(3922341057133045639)
XLA Ops:
  0.0 67.8 %fusion = f32[2,1024,3200]{2,1,0:T(8,128)} fusion(bf16[1,2,4096,3200]{3,2,1,0:T(8,128)(2,1)} %param.1, bf16[1,2,4096,1024]{3,2,1,0:T(8,128)(2,1)} %param), kind=kOutput, calls=%fused_computation | convolution fusion | flops 53687091200 | bytes 95420416 | tf_op jit(solution)/rsntd,rsntf->rndf/dot_general | solution.py:10
  67.8 421.1 %all-reduce.2 = bf16[2,1024,3200]{2,1,0:T(8,128)(2,1)} all-reduce(f32[2,1024,3200]{2,1,0:T(8,128)} %fusion), channel_id=1, replica_groups=mesh['axis_0'=32] {'axis_0'}, use_global_device_ids=true, to_apply=%add.clone | all-reduce | flops 6553600 | bytes 39321600 | tf_op jit(solution)/rsntd,rsntf->rndf/dot_general | solution.py:10
where the time goes:
time: 489 us
  blocking collectives  421 us (86%)
  matrix products  67.8 us (14%)
    dot_general x1, blocking collectives, step(): jnp.einsum('rsntd,rsntf->rndf', a, g, preferred_element_type=jnp.float32)  421 us
    dot_general x1, matrix products, step(): jnp.einsum('rsntd,rsntf->rndf', a, g, preferred_element_type=jnp.float32)  67.8 us

commit v1 on v0

v1 whole, which is shorter than its diff:
```python
import functools

import jax
import jax.numpy as jnp
from jax import lax
from jax.experimental import pallas as pl
from jax.experimental.pallas import tpu as pltpu
from jax.sharding import PartitionSpec as P

W = 256
RING = 8
MESH = pl.DeviceIdType.MESH
F32, BF16 = jnp.float32, jnp.bfloat16
HOP = 2

O_D2D = 1
O_A = O_D2D + HOP
O_Z1, O_Z2, O_Z3 = O_A + HOP, O_A + 2 * HOP, O_A + 3 * HOP
O_B = O_Z3 + HOP
O_BG = O_B + HOP
O_ZG1, O_ZG2, O_ZG3 = O_BG + HOP, O_BG + 2 * HOP, O_BG + 3 * HOP
O_AG = O_ZG3 + HOP
O_DG = O_AG + 1
O_OUT = O_DG + 2
KEEP = O_B - O_D2D + 1


def kernel(full, a_hbm, g_hbm, out_hbm, a_v, g_v, acc, keep, res, d_send, d_recv, a_send, a_recv, zr_send, zr_recv, zl_send, zl_recv,
           b_send, b_recv, in_sem, out_sem, s_sem, r_sem, zs_sem, zr_sem):
    chunks = 2 * full + 1
    rows = acc.shape[1]
    half, quarter, block, piece = rows // 2, rows // 4, rows // 16, rows // 32
    me = lax.axis_index("dp")
    x, y, z, core = me // 16, (me // 8) % 2, (me // 2) % 4, me % 2

    def dev(x, y, z, core):
        return {"dp": ((x * 2 + y) * 4 + z) * 2 + core}

    partner = dev(x, y, z, 1 - core)
    first = 1 - core
    a_at = first * x + core * y
    b_at = first * y + core * x
    a_dev = dev(x + first * (1 - 2 * x), y + core * (1 - 2 * y), z, core)
    b_dev = dev(x + core * (1 - 2 * x), y + first * (1 - 2 * y), z, core)
    right, left = dev(x, y, z + 1, core), dev(x, y, z - 1, core)

    def at(start, size):
        return pl.ds(pl.multiple_of(start, size), size)

    def remote(src, dst, send, recv, to):
        return pltpu.make_async_remote_copy(src, dst, send, recv, device_id=to, device_id_type=MESH)

    def g_copies(i, slot):
        m = (i > full).astype(jnp.int32)
        start = pl.multiple_of((i - m * (full + 1)) * W, W)
        return pltpu.make_async_copy(g_hbm.at[0, m, :, pl.ds(start, W)], g_v.at[slot], in_sem.at[slot])

    def g_mixed(m, slot):
        return pltpu.make_async_copy(
            g_hbm.at[0, m, :, pl.ds(full * W, W // 2)], g_v.at[slot, :, pl.ds(m * (W // 2), W // 2)], in_sem.at[3 + m]
        )

    def g_start(i, slot):
        @pl.when(i != full)
        def _():
            g_copies(i, slot).start()

        @pl.when(i == full)
        def _():
            g_mixed(0, slot).start()
            g_mixed(1, slot).start()

    def a_copy(m):
        return pltpu.make_async_copy(a_hbm.at[0, m], a_v.at[m], in_sem.at[5 + m])

    a_copy(0).start()
    for i in range(3):
        g_start(jnp.int32(i), i)
    a_copy(1).start()

    barrier = pltpu.get_barrier_semaphore()
    for to in (partner, a_dev, b_dev):
        pl.semaphore_signal(barrier, inc=1, device_id=to, device_id_type=MESH)

    @pl.when(z < 3)
    def _():
        pl.semaphore_signal(barrier, inc=1, device_id=right, device_id_type=MESH)

    @pl.when(z > 0)
    def _():
        pl.semaphore_signal(barrier, inc=1, device_id=left, device_id_type=MESH)

    pl.semaphore_wait(barrier, 3 + (z < 3).astype(jnp.int32) + (z > 0).astype(jnp.int32))
    a_copy(0).wait()

    def pair(k, i, src, dst, to):
        s = lax.rem(i, RING)
        return remote(src, dst, s_sem.at[k, s], r_sem.at[k, s], to)

    def d_copy(i):
        s = lax.rem(i, RING)
        return pair(0, i, d_send.at[s], d_recv.at[s], partner)

    def a_copy_out(i):
        s = lax.rem(i, RING)
        return pair(1, i, a_send.at[s], a_recv.at[s], a_dev)

    def b_copy(i):
        s = lax.rem(i, RING)
        return pair(2, i, b_send.at[s], b_recv.at[s], b_dev)

    mine_a = core * half + a_at * quarter
    mine_z = mine_a + z * block
    mine_b = mine_z + b_at * piece

    def bg_copy(i):
        ref = res.at[i, at(mine_b, piece)]
        return pair(3, i, ref, ref, b_dev)

    def ag_copy(i):
        ref = res.at[i, at(mine_a, quarter)]
        return pair(4, i, ref, ref, a_dev)

    def dg_copy(i):
        ref = res.at[i, at(core * half, half)]
        return pair(5, i, ref, ref, partner)

    def z_copy(i, way, lo, hi):
        s = lax.rem(i, RING)
        send, recv, to = ((zr_send, zr_recv, right), (zl_send, zl_recv, left))[way]
        there = pl.ds(lo * block, (hi - lo) * block)
        return remote(send.at[s, there], recv.at[s, there], zs_sem.at[way, s], zr_sem.at[way, s], to)

    def zg_copy(i, way, hop):
        s = lax.rem(i, RING)
        owner = z - (hop - 1) if way == 0 else z + (hop - 1)
        ref = res.at[i, at(mine_a + owner * block, block)]
        k = 2 + way * 3 + hop - 1
        return remote(ref, ref, zs_sem.at[k, s], zr_sem.at[k, s], (right, left)[way])

    def stage(step, offset, body):
        i = step - offset

        @pl.when((i >= 0) & (i < chunks))
        def _():
            body(i)

    def multiply(i):
        slot = lax.rem(i, 3)
        now = lax.rem(i, 2)
        dims = (((0,), (0,)), ((), ()))

        @pl.when(i != full)
        def _():
            m = (i > full).astype(jnp.int32)

            g_copies(i, slot).wait()
            acc[now] = lax.dot_general(a_v[m], g_v[slot], dims, preferred_element_type=F32)

        @pl.when(i == full)
        def _():
            a_copy(1).wait()
            for m in range(2):
                g_mixed(m, slot).wait()
                part = pl.ds(m * (W // 2), W // 2)
                acc[now, :, part] = lax.dot_general(a_v[m], g_v[slot, :, part], dims, preferred_element_type=F32)

        @pl.when(i + 3 < chunks)
        def _():
            g_start(i + 3, slot)

        d_send[lax.rem(i, RING)] = acc[now, at((1 - core) * half, half)].astype(BF16)
        d_copy(i).start()

    def on_d2d(i):
        d_copy(i).wait()
        s, k, now = lax.rem(i, RING), lax.rem(i, KEEP), lax.rem(i, 2)

        def total(which):
            here = at(core * half + which * quarter, quarter)
            return acc[now, here] + d_recv[s, at(which * quarter, quarter)].astype(F32)

        a_send[s] = total(1 - a_at).astype(BF16)
        a_copy_out(i).start()
        keep[k] = total(a_at)

    def on_a(i):
        a_copy_out(i).wait()
        s, k = lax.rem(i, RING), lax.rem(i, KEEP)
        keep[k] += a_recv[s].astype(F32)

        @pl.when(z == 0)
        def _():
            there = pl.ds(block, 3 * block)
            zr_send[s, there] = keep[k, there].astype(BF16)
            z_copy(i, 0, 1, 4).start()

        @pl.when(z == 3)
        def _():
            there = pl.ds(0, 3 * block)
            zl_send[s, there] = keep[k, there].astype(BF16)
            z_copy(i, 1, 0, 3).start()

    def pass_on(i, way, at_z):
        s, k = lax.rem(i, RING), lax.rem(i, KEEP)
        send, recv = ((zr_send, zr_recv), (zl_send, zl_recv))[way]
        lo, hi = ((at_z, 4), (0, at_z + 1))[way]

        @pl.when(z == at_z)
        def _():
            z_copy(i, way, lo, hi).wait_recv()
            lo2, hi2 = ((at_z + 1, 4), (0, at_z))[way]
            if lo2 < hi2:
                beyond = pl.ds(lo2 * block, (hi2 - lo2) * block)
                send[s, beyond] = (keep[k, beyond] + recv[s, beyond].astype(F32)).astype(BF16)
                z_copy(i, way, lo2, hi2).start()
            here = pl.ds(at_z * block, block)
            keep[k, here] += recv[s, here].astype(F32)

    def sent(i, way, at_z):
        lo, hi = ((at_z + 1, 4), (0, at_z))[way]

        @pl.when(z == at_z)
        def _():
            z_copy(i, way, lo, hi).wait_send()

    def on_z1(i):
        sent(i, 0, 0)
        sent(i, 1, 3)
        pass_on(i, 0, 1)
        pass_on(i, 1, 2)

    def on_z2(i):
        sent(i, 0, 1)
        sent(i, 1, 2)
        pass_on(i, 0, 2)
        pass_on(i, 1, 1)

    def on_z3(i):
        sent(i, 0, 2)
        sent(i, 1, 1)
        pass_on(i, 0, 3)
        pass_on(i, 1, 0)
        s, k = lax.rem(i, RING), lax.rem(i, KEEP)
        b_send[s] = keep[k, at(z * block + (1 - b_at) * piece, piece)].astype(BF16)
        b_copy(i).start()

    def on_b(i):
        b_copy(i).wait()
        s, k = lax.rem(i, RING), lax.rem(i, KEEP)
        total = keep[k, at(z * block + b_at * piece, piece)] + b_recv[s].astype(F32)
        res[i, at(mine_b, piece)] = total.astype(BF16)
        bg_copy(i).start()

    def can(way, hop):
        return (z >= hop - 1) & (z < 3) if way == 0 else (z <= 4 - hop) & (z > 0)

    def gets(way, hop):
        return z >= hop if way == 0 else z <= 3 - hop

    def gather(i, hop):
        for way in range(2):
            if hop > 0:

                @pl.when(gets(way, hop))
                def _():
                    zg_copy(i, way, hop).wait_recv()

            if hop < 3:

                @pl.when(can(way, hop + 1))
                def _():
                    zg_copy(i, way, hop + 1).start()

            if hop > 0:

                @pl.when(can(way, hop))
                def _():
                    zg_copy(i, way, hop).wait_send()

    def on_bg(i):
        bg_copy(i).wait()
        gather(i, 0)

    def on_zg3(i):
        gather(i, 3)
        ag_copy(i).start()

    def on_ag(i):
        ag_copy(i).wait()
        dg_copy(i).start()

    def out_copy(i):
        m = (i > full).astype(jnp.int32)
        start = pl.multiple_of((i - m * (full + 1)) * W, W)
        return pltpu.make_async_copy(res.at[i], out_hbm.at[m, :, pl.ds(start, W)], out_sem.at[lax.rem(i, 4)])

    def out_mixed(i, m):
        part = pl.ds(m * (W // 2), W // 2)
        return pltpu.make_async_copy(res.at[i, :, part], out_hbm.at[m, :, pl.ds(full * W, W // 2)], out_sem.at[4 + m])

    def on_dg(i):
        dg_copy(i).wait()

        @pl.when(i != full)
        def _():
            out_copy(i).start()

        @pl.when(i == full)
        def _():
            out_mixed(i, 0).start()
            out_mixed(i, 1).start()

    def on_out(i):
        @pl.when(i != full)
        def _():
            out_copy(i).wait()

        @pl.when(i == full)
        def _():
            out_mixed(i, 0).wait()
            out_mixed(i, 1).wait()

    @pl.loop(0, chunks + O_OUT)
    def _(step):
        stage(step, 0, multiply)
        stage(step, O_D2D, on_d2d)
        stage(step, O_A, on_a)
        stage(step, O_Z1, on_z1)
        stage(step, O_Z2, on_z2)
        stage(step, O_Z3, on_z3)
        stage(step, O_B, on_b)
        stage(step, O_BG, on_bg)
        stage(step, O_ZG1, lambda i: gather(i, 1))
        stage(step, O_ZG2, lambda i: gather(i, 2))
        stage(step, O_ZG3, on_zg3)
        stage(step, O_AG, on_ag)
        stage(step, O_DG, on_dg)
        stage(step, O_OUT, on_out)


def solution(mesh):
    def step(a, g):
        _, mats, tokens, rows = a.shape
        cols = g.shape[-1]
        full = cols // W
        chunks = 2 * full + 1
        half, quarter, piece = rows // 2, rows // 4, rows // 32
        hbm = pl.BlockSpec(memory_space=pl.ANY)
        ring = lambda n: pltpu.VMEM((RING, n, W), BF16)
        return pl.pallas_call(
            functools.partial(kernel, full),
            out_shape=jax.ShapeDtypeStruct((mats, rows, cols), BF16),
            in_specs=[hbm, hbm],
            out_specs=hbm,
            scratch_shapes=[
                pltpu.VMEM((mats, tokens, rows), BF16),
                pltpu.VMEM((3, tokens, W), BF16),
                pltpu.VMEM((2, rows, W), F32),
                pltpu.VMEM((KEEP, quarter, W), F32),
                pltpu.VMEM((chunks, rows, W), BF16),
                ring(half),
                ring(half),
                *[ring(quarter)] * 6,
                ring(piece),
                ring(piece),
                pltpu.SemaphoreType.DMA((7,)),
                pltpu.SemaphoreType.DMA((6,)),
                pltpu.SemaphoreType.DMA((6, RING)),
                pltpu.SemaphoreType.DMA((6, RING)),
                pltpu.SemaphoreType.DMA((8, RING)),
                pltpu.SemaphoreType.DMA((8, RING)),
            ],
            compiler_params=pltpu.CompilerParams(
                collective_id=0, has_side_effects=True, vmem_limit_bytes=62 * 1024 * 1024
            ),
        )(a, g)

    return jax.shard_map(
        step, mesh=mesh, in_specs=(P(("rep", "dp")), P(("rep", "dp"))), out_specs=P("rep"), check_vma=False
    )
```

time: 489 us -> 145 us (0.30)
  blocking collectives: 421 us -> 0 us
  Pallas kernels: 0 us -> 134 us
  matrix products: 67.8 us -> 0 us
  local copies, waits for them, and re-layouts: 0 us -> 10.8 us
    dot_general x1 -> x0, blocking collectives: 421 us -> none  [step(): jnp.einsum('rsntd,rsntf->rndf', a, g, preferred_element_type=jnp.float32)]
    pallas_call x0 -> x1, Pallas kernels: none -> 134 us  [step(): pl.pallas_call(functools.partial(kernel, full), out_shape=jax.ShapeDtypeS...]
    dot_general x1 -> x0, matrix products: 67.8 us -> none  [step(): jnp.einsum('rsntd,rsntf->rndf', a, g, preferred_element_type=jnp.float32)]
    unnamed x0 -> x1, local copies, waits for them, and re-layouts: none -> 10.8 us
where the time goes in v1:
time: 145 us
  Pallas kernels  134 us (92%)
  local copies, waits for them, and re-layouts  10.8 us (7%)
    pallas_call x1, Pallas kernels, step(): pl.pallas_call(functools.partial(kernel, full), out_shape=jax.ShapeDtypeS...  134 us
    unnamed x1, local copies, waits for them, and re-layouts  10.8 us

profile of v1, /device:TPU:0, one launch (start us, length us, event | category | flops | bytes accessed | tf_op | source)
XLA Modules:
  0.0 145.2 jit_solution(4481979114548661819)
XLA Ops:
  0.0 134.4 %shard_map.28 = bf16[2,1024,3200]{2,1,0:T(8,128)(2,1)} custom-call(bf16[1,2,4096,1024]{3,2,1,0:T(8,128)(2,1)} %a_hbm.1, bf16[1,2,4096,3200]{3,2,1,0:T(8,128)(2,1)} %g_hbm.1), custom_call_target="tpu_custom_call" | custom-call | tf_op jit(solution)/shard_map/pallas_call | solution.py:351
  134.4 10.8 %copy.4 = bf16[2,1024,3200]{2,1,0:T(8,128)(2,1)} copy(bf16[2,1024,3200]{2,1,0:T(8,128)(2,1)} %shard_map.28) | data formatting | bytes 26214400

commit v2 on v1

--- a/solution.py
+++ b/solution.py
@@ -1,4 +1,5 @@
 import functools
+import itertools
 
 import jax
 import jax.numpy as jnp
@@ -11,25 +12,17 @@
 RING = 8
 MESH = pl.DeviceIdType.MESH
 F32, BF16 = jnp.float32, jnp.bfloat16
-HOP = 2
-
-O_D2D = 1
-O_A = O_D2D + HOP
-O_Z1, O_Z2, O_Z3 = O_A + HOP, O_A + 2 * HOP, O_A + 3 * HOP
-O_B = O_Z3 + HOP
-O_BG = O_B + HOP
-O_ZG1, O_ZG2, O_ZG3 = O_BG + HOP, O_BG + 2 * HOP, O_BG + 3 * HOP
-O_AG = O_ZG3 + HOP
-O_DG = O_AG + 1
-O_OUT = O_DG + 2
-KEEP = O_B - O_D2D + 1
-
-
-def kernel(full, a_hbm, g_hbm, out_hbm, a_v, g_v, acc, keep, res, d_send, d_recv, a_send, a_recv, zr_send, zr_recv, zl_send, zl_recv,
-           b_send, b_recv, in_sem, out_sem, s_sem, r_sem, zs_sem, zr_sem):
+
+LAGS = dict(d2d=1, a=3, z1=3, z2=3, z3=3, b=3, zg1=3, zg2=3, zg3=5, ag=6, dg=2)
+AT = dict(zip(LAGS, itertools.accumulate(LAGS.values())))
+KEEP = (AT["b"] - AT["d2d"]) // 2 + 1
+
+
+def kernel(full, a_hbm, g_hbm, res, a_v, g_v, acc, keep, d_send, d_recv, a_send, a_recv, zr_send, zr_recv, zl_send, zl_recv,
+           b_send, b_recv, in_sem, s_sem, r_sem, zs_sem, zr_sem):
     chunks = 2 * full + 1
-    rows = acc.shape[1]
-    half, quarter, block, piece = rows // 2, rows // 4, rows // 16, rows // 32
+    rows = 2 * acc.shape[1]
+    half, quarter, block = rows // 2, rows // 4, rows // 16
     me = lax.axis_index("dp")
     x, y, z, core = me // 16, (me // 8) % 2, (me // 2) % 4, me % 2
 
@@ -39,7 +32,6 @@
     partner = dev(x, y, z, 1 - core)
     first = 1 - core
     a_at = first * x + core * y
-    b_at = first * y + core * x
     a_dev = dev(x + first * (1 - 2 * x), y + core * (1 - 2 * y), z, core)
     b_dev = dev(x + core * (1 - 2 * x), y + first * (1 - 2 * y), z, core)
     right, left = dev(x, y, z + 1, core), dev(x, y, z - 1, core)
@@ -111,19 +103,14 @@
 
     mine_a = core * half + a_at * quarter
     mine_z = mine_a + z * block
-    mine_b = mine_z + b_at * piece
-
-    def bg_copy(i):
-        ref = res.at[i, at(mine_b, piece)]
-        return pair(3, i, ref, ref, b_dev)
 
     def ag_copy(i):
         ref = res.at[i, at(mine_a, quarter)]
-        return pair(4, i, ref, ref, a_dev)
+        return pair(3, i, ref, ref, a_dev)
 
     def dg_copy(i):
         ref = res.at[i, at(core * half, half)]
-        return pair(5, i, ref, ref, partner)
+        return pair(4, i, ref, ref, partner)
 
     def z_copy(i, way, lo, hi):
         s = lax.rem(i, RING)
@@ -138,47 +125,68 @@
         k = 2 + way * 3 + hop - 1
         return remote(ref, ref, zs_sem.at[k, s], zr_sem.at[k, s], (right, left)[way])
 
-    def stage(step, offset, body):
-        i = step - offset
-
-        @pl.when((i >= 0) & (i < chunks))
-        def _():
-            body(i)
-
-    def multiply(i):
+    def stage(step, part, name, body):
+        if AT[name] % 2 == part:
+            i = step - AT[name] // 2
+
+            @pl.when((i >= 0) & (i < chunks))
+            def _():
+                body(i)
+
+    def product(i, slot, cols, put):
+        dims = (((0,), (0,)), ((), ()))
+
+        @pl.when(i != full)
+        def _():
+            m = (i > full).astype(jnp.int32)
+            put(pl.ds(0, W), lax.dot_general(a_v[m, :, cols], g_v[slot], dims, preferred_element_type=F32))
+
+        @pl.when(i == full)
+        def _():
+            for m in range(2):
+                part = pl.ds(m * (W // 2), W // 2)
+                put(part, lax.dot_general(a_v[m, :, cols], g_v[slot, :, part], dims, preferred_element_type=F32))
+
+    def multiply_other(i):
+        slot = lax.rem(i, 3)
+        s = lax.rem(i, RING)
+
+        @pl.when(i != full)
+        def _():
+            g_copies(i, slot).wait()
+
+        @pl.when(i == full)
+        def _():
+            a_copy(1).wait()
+            g_mixed(0, slot).wait()
+            g_mixed(1, slot).wait()
+
+        def put(part, sums):
+            d_send[s, :, part] = sums.astype(BF16)
+
+        product(i, slot, at((1 - core) * half, half), put)
+        d_copy(i).start()
+
+    def multiply_mine(i):
         slot = lax.rem(i, 3)
         now = lax.rem(i, 2)
-        dims = (((0,), (0,)), ((), ()))
-
-        @pl.when(i != full)
-        def _():
-            m = (i > full).astype(jnp.int32)
-
-            g_copies(i, slot).wait()
-            acc[now] = lax.dot_general(a_v[m], g_v[slot], dims, preferred_element_type=F32)
-
-        @pl.when(i == full)
-        def _():
-            a_copy(1).wait()
-            for m in range(2):
-                g_mixed(m, slot).wait()
-                part = pl.ds(m * (W // 2), W // 2)
-                acc[now, :, part] = lax.dot_general(a_v[m], g_v[slot, :, part], dims, preferred_element_type=F32)
+
+        def put(part, sums):
+            acc[now, :, part] = sums
+
+        product(i, slot, at(core * half, half), put)
 
         @pl.when(i + 3 < chunks)
         def _():
             g_start(i + 3, slot)
-
-        d_send[lax.rem(i, RING)] = acc[now, at((1 - core) * half, half)].astype(BF16)
-        d_copy(i).start()
 
     def on_d2d(i):
         d_copy(i).wait()
         s, k, now = lax.rem(i, RING), lax.rem(i, KEEP), lax.rem(i, 2)
 
         def total(which):
-            here = at(core * half + which * quarter, quarter)
-            return acc[now, here] + d_recv[s, at(which * quarter, quarter)].astype(F32)
+            here = at(which * quarter, quarter)
+            return acc[now, here] + d_recv[s, here].astype(F32)
 
         a_send[s] = total(1 - a_at).astype(BF16)
         a_copy_out(i).start()
@@ -242,15 +250,15 @@
         pass_on(i, 0, 3)
         pass_on(i, 1, 0)
         s, k = lax.rem(i, RING), lax.rem(i, KEEP)
-        b_send[s] = keep[k, at(z * block + (1 - b_at) * piece, piece)].astype(BF16)
+        b_send[s] = keep[k, at(z * block, block)].astype(BF16)
         b_copy(i).start()
 
     def on_b(i):
         b_copy(i).wait()
-        s, k = lax.rem(i, RING), lax.rem(i, KEEP)
-        total = keep[k, at(z * block + b_at * piece, piece)] + b_recv[s].astype(F32)
-        res[i, at(mine_b, piece)] = total.astype(BF16)
-        bg_copy(i).start()
+        s = lax.rem(i, RING)
+        total = b_send[s].astype(F32) + b_recv[s].astype(F32)
+        res[i, at(mine_z, block)] = total.astype(BF16)
+        gather(i, 0)
 
     def can(way, hop):
         return (z >= hop - 1) & (z < 3) if way == 0 else (z <= 4 - hop) & (z > 0)
@@ -278,10 +286,6 @@
                 def _():
                     zg_copy(i, way, hop).wait_send()
 
-    def on_bg(i):
-        bg_copy(i).wait()
-        gather(i, 0)
-
     def on_zg3(i):
         gather(i, 3)
         ag_copy(i).start()
@@ -290,53 +294,45 @@
         ag_copy(i).wait()
         dg_copy(i).start()
 
-    def out_copy(i):
-        m = (i > full).astype(jnp.int32)
-        start = pl.multiple_of((i - m * (full + 1)) * W, W)
-        return pltpu.make_async_copy(res.at[i], out_hbm.at[m, :, pl.ds(start, W)], out_sem.at[lax.rem(i, 4)])
-
-    def out_mixed(i, m):
-        part = pl.ds(m * (W // 2), W // 2)
-        return pltpu.make_async_copy(res.at[i, :, part], out_hbm.at[m, :, pl.ds(full * W, W // 2)], out_sem.at[4 + m])
-
     def on_dg(i):
         dg_copy(i).wait()
 
-        @pl.when(i != full)
-        def _():
-            out_copy(i).start()
-
-        @pl.when(i == full)
-        def _():
-            out_mixed(i, 0).start()
-            out_mixed(i, 1).start()
-
-    def on_out(i):
-        @pl.when(i != full)
-        def _():
-            out_copy(i).wait()
-
-        @pl.when(i == full)
-        def _():
-            out_mixed(i, 0).wait()
-            out_mixed(i, 1).wait()
-
-    @pl.loop(0, chunks + O_OUT)
+    @pl.loop(0, chunks + (AT["dg"] + 1) // 2)
     def _(step):
-        stage(step, 0, multiply)
-        stage(step, O_D2D, on_d2d)
-        stage(step, O_A, on_a)
-        stage(step, O_Z1, on_z1)
-        stage(step, O_Z2, on_z2)
-        stage(step, O_Z3, on_z3)
-        stage(step, O_B, on_b)
-        stage(step, O_BG, on_bg)
-        stage(step, O_ZG1, lambda i: gather(i, 1))
-        stage(step, O_ZG2, lambda i: gather(i, 2))
-        stage(step, O_ZG3, on_zg3)
-        stage(step, O_AG, on_ag)
-        stage(step, O_DG, on_dg)
-        stage(step, O_OUT, on_out)
+        for part in range(2):
+
+            @pl.when(step < chunks)
+            def _():
+                (multiply_other, multiply_mine)[part](step)
+
+            stage(step, part, "d2d", on_d2d)
+            stage(step, part, "a", on_a)
+            stage(step, part, "z1", on_z1)
+            stage(step, part, "z2", on_z2)
+            stage(step, part, "z3", on_z3)
+            stage(step, part, "b", on_b)
+            stage(step, part, "zg1", lambda i: gather(i, 1))
+            stage(step, part, "zg2", lambda i: gather(i, 2))
+            stage(step, part, "zg3", on_zg3)
+            stage(step, part, "ag", on_ag)
+            stage(step, part, "dg", on_dg)
+
+
+def place(full, blocks, out, sem):
+    chunks = 2 * full + 1
+    copies = []
+    for m in range(2):
+        for j in range(full):
+            i = m * (full + 1) + j
+            copies.append(pltpu.make_async_copy(blocks.at[i], out.at[m, :, pl.ds(j * W, W)], sem.at[i]))
+        part = pl.ds(m * (W // 2), W // 2)
+        copies.append(
+            pltpu.make_async_copy(blocks.at[full, :, part], out.at[m, :, pl.ds(full * W, W // 2)], sem.at[full + m * (full + 1)])
+        )
+    for c in copies:
+        c.start()
+    for c in copies:
+        c.wait()
 
 
 def solution(mesh):
@@ -345,36 +341,42 @@
         cols = g.shape[-1]
         full = cols // W
         chunks = 2 * full + 1
-        half, quarter, piece = rows // 2, rows // 4, rows // 32
+        half, quarter, block = rows // 2, rows // 4, rows // 16
         hbm = pl.BlockSpec(memory_space=pl.ANY)
         ring = lambda n: pltpu.VMEM((RING, n, W), BF16)
-        return pl.pallas_call(
+        blocks = pl.pallas_call(
             functools.partial(kernel, full),
-            out_shape=jax.ShapeDtypeStruct((mats, rows, cols), BF16),
+            out_shape=pltpu.VMEM((chunks, rows, W), BF16),
             in_specs=[hbm, hbm],
-            out_specs=hbm,
+            out_specs=pl.BlockSpec(memory_space=pltpu.VMEM),
             scratch_shapes=[
                 pltpu.VMEM((mats, tokens, rows), BF16),
                 pltpu.VMEM((3, tokens, W), BF16),
-                pltpu.VMEM((2, rows, W), F32),
+                pltpu.VMEM((2, half, W), F32),
                 pltpu.VMEM((KEEP, quarter, W), F32),
-                pltpu.VMEM((chunks, rows, W), BF16),
                 ring(half),
                 ring(half),
                 *[ring(quarter)] * 6,
-                ring(piece),
-                ring(piece),
+                ring(block),
+                ring(block),
                 pltpu.SemaphoreType.DMA((7,)),
-                pltpu.SemaphoreType.DMA((6,)),
-                pltpu.SemaphoreType.DMA((6, RING)),
-                pltpu.SemaphoreType.DMA((6, RING)),
+                pltpu.SemaphoreType.DMA((5, RING)),
+                pltpu.SemaphoreType.DMA((5, RING)),
                 pltpu.SemaphoreType.DMA((8, RING)),
                 pltpu.SemaphoreType.DMA((8, RING)),
             ],
             compiler_params=pltpu.CompilerParams(
-                collective_id=0, has_side_effects=True, vmem_limit_bytes=62 * 1024 * 1024
+                collective_id=0, has_side_effects=True, vmem_limit_bytes=48 * 1024 * 1024
             ),
         )(a, g)
+        return pl.pallas_call(
+            functools.partial(place, full),
+            out_shape=jax.ShapeDtypeStruct((mats, rows, cols), BF16),
+            in_specs=[pl.BlockSpec(memory_space=pltpu.VMEM)],
+            out_specs=hbm,
+            scratch_shapes=[pltpu.SemaphoreType.DMA((chunks + 1,))],
+            compiler_params=pltpu.CompilerParams(vmem_limit_bytes=16 * 1024 * 1024),
+        )(blocks)
 
     return jax.shard_map(
         step, mesh=mesh, in_specs=(P(("rep", "dp")), P(("rep", "dp"))), out_specs=P("rep"), check_vma=False

time: 145 us -> 128 us (0.88)
  local copies, waits for them, and re-layouts: 10.8 us -> 0 us
  Pallas kernels: 134 us -> 128 us
    unnamed x1 -> x0, local copies, waits for them, and re-layouts: 10.8 us -> none
    pallas_call x1 -> x2, Pallas kernels: 134 us -> 128 us  [the longest x1 123 us: step(): pl.pallas_call(functools.partial(kernel, full), out_shape=pltpu.VMEM((chu...]
where the time goes in v2:
time: 128 us
  Pallas kernels  128 us (100%)
    pallas_call x1, Pallas kernels, step(): pl.pallas_call(functools.partial(kernel, full), out_shape=pltpu.VMEM((chu...  123 us
    pallas_call x1, Pallas kernels, step(): pl.pallas_call(functools.partial(place, full), out_shape=jax.ShapeDtypeSt...  4.91 us

profile of v2, /device:TPU:0, one launch (start us, length us, event | category | flops | bytes accessed | tf_op | source)
XLA Modules:
  0.0 128.1 jit_solution(4164989108364748676)
XLA Ops:
  0.0 123.2 %shard_map.28.blocks = bf16[25,1024,256]{2,1,0:T(8,128)(2,1)S(1)} custom-call(bf16[1,2,4096,1024]{3,2,1,0:T(8,128)(2,1)} %a_hbm.1, bf16[1,2,4096,3200]{3,2,1,0:T(8,128)(2,1)} %g_hbm.1), custom_call_target="tpu_custom_call" | custom-call | tf_op jit(solution)/shard_map/pallas_call | solution.py:347
  123.2 4.9 %shard_map.29 = bf16[2,1024,3200]{2,1,0:T(8,128)(2,1)} custom-call(bf16[25,1024,256]{2,1,0:T(8,128)(2,1)S(1)} %shard_map.28.blocks), custom_call_target="tpu_custom_call" | custom-call | tf_op jit(solution)/shard_map/pallas_call | solution.py:372

commit v3 on v2

--- a/solution.py
+++ b/solution.py
@@ -62,13 +62,13 @@
             g_mixed(0, slot).start()
             g_mixed(1, slot).start()
 
-    def a_copy(m):
-        return pltpu.make_async_copy(a_hbm.at[0, m], a_v.at[m], in_sem.at[5 + m])
-
-    a_copy(0).start()
-    for i in range(3):
-        g_start(jnp.int32(i), i)
-    a_copy(1).start()
+    other_cols, my_cols = at((1 - core) * half, half), at(core * half, half)
+
+    def a_copy(m, cols, k):
+        return pltpu.make_async_copy(a_hbm.at[0, m, :, cols], a_v.at[m, :, cols], in_sem.at[5 + 2 * m + k])
+
+    a_copy(0, other_cols, 0).start()
+    g_start(jnp.int32(0), 0)
 
     barrier = pltpu.get_barrier_semaphore()
     for to in (partner, a_dev, b_dev):
@@ -83,7 +83,10 @@
         pl.semaphore_signal(barrier, inc=1, device_id=left, device_id_type=MESH)
 
     pl.semaphore_wait(barrier, 3 + (z < 3).astype(jnp.int32) + (z > 0).astype(jnp.int32))
-    a_copy(0).wait()
+    a_copy(0, my_cols, 1).start()
+    g_start(jnp.int32(1), 1)
+    g_start(jnp.int32(2), 2)
+    a_copy(0, other_cols, 0).wait()
 
     def pair(k, i, src, dst, to):
         s = lax.rem(i, RING)
@@ -145,7 +148,7 @@
         def _():
             for m in range(2):
                 part = pl.ds(m * (W // 2), W // 2)
-                put(part, lax.dot_general(a_v[m, :, cols], g_v[slot, :, part], dims, preferred_element_type=F32))
+                put(part, lax.dot_general(g_v[slot, :, part], a_v[m, :, cols], dims, preferred_element_type=F32).T)
 
     def multiply_other(i):
         slot = lax.rem(i, 3)
@@ -157,14 +160,15 @@
 
         @pl.when(i == full)
         def _():
-            a_copy(1).wait()
+            a_copy(1, other_cols, 0).wait()
+            a_copy(1, my_cols, 1).wait()
             g_mixed(0, slot).wait()
             g_mixed(1, slot).wait()
 
         def put(part, sums):
             d_send[s, :, part] = sums.astype(BF16)
 
-        product(i, slot, at((1 - core) * half, half), put)
+        product(i, slot, other_cols, put)
         d_copy(i).start()
 
     def multiply_mine(i):
@@ -174,7 +178,16 @@
         def put(part, sums):
             acc[now, :, part] = sums
 
-        product(i, slot, at(core * half, half), put)
+        @pl.when(i == 0)
+        def _():
+            a_copy(0, my_cols, 1).wait()
+
+        @pl.when(i == 1)
+        def _():
+            a_copy(1, other_cols, 0).start()
+            a_copy(1, my_cols, 1).start()
+
+        product(i, slot, my_cols, put)
 
         @pl.when(i + 3 < chunks)
         def _():
@@ -359,7 +372,7 @@
                 *[ring(quarter)] * 6,
                 ring(block),
                 ring(block),
-                pltpu.SemaphoreType.DMA((7,)),
+                pltpu.SemaphoreType.DMA((9,)),
                 pltpu.SemaphoreType.DMA((5, RING)),
                 pltpu.SemaphoreType.DMA((5, RING)),
                 pltpu.SemaphoreType.DMA((8, RING)),

time: 128 us -> 125 us (0.977)
  Pallas kernels: 128 us -> 125 us
    pallas_call x1, Pallas kernels: 123 us -> 120 us  [step(): pl.pallas_call(functools.partial(kernel, full), out_shape=pltpu.VMEM((chu...]
where the time goes in v3:
time: 125 us
  Pallas kernels  125 us (100%)
    pallas_call x1, Pallas kernels, step(): pl.pallas_call(functools.partial(kernel, full), out_shape=pltpu.VMEM((chu...  120 us
    pallas_call x1, Pallas kernels, step(): pl.pallas_call(functools.partial(place, full), out_shape=jax.ShapeDtypeSt...  4.91 us

profile of v3, /device:TPU:0, one launch (start us, length us, event | category | flops | bytes accessed | tf_op | source)
XLA Modules:
  0.0 124.9 jit_solution(7657986810805347645)
XLA Ops:
  0.0 120.0 %shard_map.28.blocks = bf16[25,1024,256]{2,1,0:T(8,128)(2,1)S(1)} custom-call(bf16[1,2,4096,1024]{3,2,1,0:T(8,128)(2,1)} %a_hbm.1, bf16[1,2,4096,3200]{3,2,1,0:T(8,128)(2,1)} %g_hbm.1), custom_call_target="tpu_custom_call" | custom-call | tf_op jit(solution)/shard_map/pallas_call | solution.py:360
  120.0 4.9 %shard_map.29 = bf16[2,1024,3200]{2,1,0:T(8,128)(2,1)} custom-call(bf16[25,1024,256]{2,1,0:T(8,128)(2,1)S(1)} %shard_map.28.blocks), custom_call_target="tpu_custom_call" | custom-call | tf_op jit(solution)/shard_map/pallas_call | solution.py:385
